TPU v7x, 32 devices: a whole 2x2x4 slice. The times are simulated.
32 devices in a mesh: cuts: 4 (over z), dev: 8 (over y, x, core).
Axes of the slice: x: 2, y: 2, z: 4, core: 2. Of those that a mesh axis runs over, the one named last changes fastest.
Arguments:
- inputs: bfloat16 [16384, 3072], P(('cuts', 'dev')), may hold values from -6 to 6
- cotangent: bfloat16 [16384, 512], P(('cuts', 'dev')), may hold values from -0.29882812 to 0.29882812
- errors: bfloat16 [32, 3072, 512], P(('cuts', 'dev')), may hold values from -6 to 6
- previous_q: float32 [512, 64], replicated, may hold values from -0.25 to 0.25
Outputs:
- new_errors: bfloat16 [32, 3072, 512], P(('cuts', 'dev'))
- p_hat: float32 [3072, 64], replicated
- q_mean: float32 [512, 64], replicated
All inputs are finite; a program needn't handle non-finite values.
Results may differ from a plain program's by a relative error of at most 0.001.
Values sent between devices are 32-bit elements; how exact they have to be, the bound alone decides.
No kernel may reach another device: no remote copies, remote signals or barrier semaphores. Data moves between devices by JAX's collectives and lax.ppermute only.
A program may use at most 64 MiB of HBM per device.

v0:
```python
import jax
import jax.numpy as jnp
from jax import lax
from jax.sharding import PartitionSpec as P

HI = lax.Precision.HIGHEST


def solve_factor(gram, p_rows):
    lower = jnp.linalg.cholesky(gram)
    return lax.linalg.triangular_solve(lower, p_rows, left_side=False, lower=True, transpose_a=True)


def contract_rows(left, right):
    return lax.dot_general(
        left, right, (((0,), (0,)), ((), ())), precision=HI, preferred_element_type=jnp.float32
    )


def body(inputs, cotangent, errors, previous_q):
    grad = lax.dot_general(
        inputs, cotangent, (((0,), (0,)), ((), ())), preferred_element_type=jnp.float32
    )
    merged = grad + errors[0].astype(jnp.float32)
    devices = lax.axis_size("cuts") * lax.axis_size("dev")
    p_share = lax.psum_scatter(
        jnp.dot(merged, previous_q, precision=HI), "dev", scatter_dimension=0, tiled=True
    )
    p_share = lax.psum(p_share, "cuts")
    gram = lax.psum(contract_rows(p_share, p_share), "dev")
    hat_share = solve_factor(gram, p_share)
    p_hat = lax.all_gather(hat_share, "dev", axis=0, tiled=True)
    q_share = lax.psum_scatter(contract_rows(merged, p_hat), "dev", scatter_dimension=0, tiled=True)
    q_share = lax.psum(q_share, "cuts")
    q_sum = lax.all_gather(q_share, "dev", axis=0, tiled=True)
    q_mean = q_sum / devices
    approx = jnp.dot(p_hat, q_mean.T, precision=HI)
    new_errors = (merged - approx).astype(jnp.bfloat16)[None]
    return (new_errors, p_hat, q_mean)


def solution(mesh):
    in_specs = (
        P(("cuts", "dev"), None),
        P(("cuts", "dev"), None),
        P(("cuts", "dev"), None, None),
        P(),
    )
    out_specs = (P(("cuts", "dev"), None, None), P(), P())
    return jax.shard_map(body, mesh=mesh, in_specs=in_specs, out_specs=out_specs, check_vma=False)
```

profile of v0, /device:TPU:0, one launch (start us, length us, event | category | flops | bytes accessed | tf_op | source)
XLA Modules:
  0.0 238.6 jit_solution(2747192408776111508)
XLA Ops:
  7.2 0.0 copy-start
  7.2 0.0 copy-start.3
  7.2 0.0 reduce-scatter.3.cloned.1.call-start
  7.2 1.8 copy-done
  9.1 4.0 %convert_add_fusion = f32[3072,512]{1,0:T(8,128)S(1)} fusion(bf16[512,3072]{1,0:T(8,128)(2,1)S(1)} %copy-done, bf16[512,512]{1,0:T(8,128)(2,1)} %param.5, bf16[1,3072,512]{2,1,0:T(8,128)(2,1)} %param.6), kind=kOutput, calls=%fused_computation | convolution fusion | flops 1613758464 | bytes 13107200 | tf_op jit(solution)/shard_map/dot_general | solution.py:21
  13.1 2.7 %copy-done.1 = f32[3072,512]{1,0:T(8,128)} copy-done((f32[3072,512]{1,0:T(8,128)}, f32[3072,512]{1,0:T(8,128)S(1)}, u32[]{:S(2)}) %copy-start.1) | copy-done | bytes 6291480
  15.7 0.0 copy-done.3
  15.7 7.1 %fusion.5 = f32[3072,64]{0,1:T(8,128)} fusion(f32[3072,512]{1,0:T(8,128)S(1)} %convert_add_fusion, f32[512,64]{0,1:T(8,128)S(1)} %copy-done.3), kind=kOutput, calls=%fused_computation.14 | convolution fusion | flops 1207959552 | bytes 7208960 | tf_op jit(solution)/shard_map/dot_general | solution.py:27
  22.8 0.0 reduce-scatter.3.cloned.1.call-update
  22.8 0.0 all-reduce.2.cloned.1.call-start
  22.9 37.8 %reduce-scatter.3.cloned.1.call-done = f32[384,64]{0,1:T(8,128)} async-done(((f32[3072,64]{0,1:T(8,128)}), f32[384,64]{0,1:T(8,128)}) %reduce-scatter.3.cloned.1.call-update) | async-done | bytes 98320 | tf_op jit(solution)/shard_map/reduce_scatter | solution.py:26
  60.6 0.0 all-reduce.2.cloned.1.call-update
  60.7 0.0 reduce-scatter.5.cloned.1.call-start
  60.7 36.7 %all-reduce.2.cloned.1.call-done = f32[384,64]{0,1:T(8,128)} async-done(((f32[384,64]{0,1:T(8,128)}), f32[384,64]{0,1:T(8,128)}) %all-reduce.2.cloned.1.call-update) | async-done | bytes 98320 | tf_op jit(solution)/shard_map/psum | solution.py:29
  97.4 1.2 fusion.6
  98.7 22.4 %psum.22 = f32[64,64]{0,1:T(8,128)S(1)} all-reduce(f32[64,64]{0,1:T(8,128)S(1)} %fusion.6), channel_id=1, replica_groups=mesh['cuts'=4,'dev'=8] {'dev'}, use_global_device_ids=true, to_apply=%region_2.0 | all-reduce | flops 4096 | bytes 32768 | tf_op jit(solution)/shard_map/psum | solution.py:30
  121.0 0.1 copy.8
  121.1 5.8 %cholesky.16 = f32[64,64]{1,0:T(8,128)S(1)} custom-call(f32[64,64]{1,0:T(8,128)S(1)} %fusion.4), custom_call_target="Cholesky" | custom-call | tf_op jit(solution)/shard_map/jit(cholesky)/cholesky | solution.py:10
  127.0 0.6 compare_reduce_fusion
  127.6 0.7 fusion.1
  128.3 4.9 %custom-call.6 = f32[1,64,64]{1,2,0:T(8,128)S(1)} custom-call(f32[1,64,64]{2,1,0:T(8,128)S(1)} %fusion.1), custom_call_target="InvertDiagBlocksLowerTriangular" | custom-call | tf_op jit(solution)/shard_map/triangular_solve | solution.py:11
  133.2 1.2 fusion.2
  134.4 11.1 %all_gather.6 = f32[3072,64]{0,1:T(8,128)S(1)} all-gather(f32[384,64]{0,1:T(8,128)S(1)} %fusion.2), channel_id=1, replica_groups=mesh['cuts'=4,'dev'=8] {'dev'}, dimensions={0}, use_global_device_ids=true | all-gather | bytes 884736 | tf_op jit(solution)/shard_map/all_gather | solution.py:32
  145.5 0.9 copy-done.2
  146.4 12.7 %fusion.7 = f32[512,64]{1,0:T(8,128)} fusion(f32[3072,512]{1,0:T(8,128)} %copy-done.1, f32[3072,64]{0,1:T(8,128)S(1)} %all_gather.6), kind=kOutput, calls=%fused_computation.16 | convolution fusion | flops 1207959552 | bytes 7208960 | tf_op jit(solution)/shard_map/dot_general | solution.py:15
  159.1 0.0 reduce-scatter.5.cloned.1.call-update
  159.1 32.7 %reduce-scatter.5.cloned.1.call-done = f32[64,64]{1,0:T(8,128)} async-done(((f32[512,64]{1,0:T(8,128)}), f32[64,64]{1,0:T(8,128)}) %reduce-scatter.5.cloned.1.call-update) | async-done | bytes 16400 | tf_op jit(solution)/shard_map/reduce_scatter | solution.py:33
  191.8 19.6 %psum.23 = f32[64,64]{1,0:T(8,128)S(1)} all-reduce(f32[64,64]{1,0:T(8,128)} %reduce-scatter.5.cloned.1.call-done), channel_id=1, replica_groups=mesh['cuts'=4,'dev'=8] {'cuts'}, use_global_device_ids=true, to_apply=%region_6.7 | all-reduce | flops 4096 | bytes 32768 | tf_op jit(solution)/shard_map/psum | solution.py:34
  211.4 9.2 %all_gather.7 = f32[512,64]{1,0:T(8,128)S(1)} all-gather(f32[64,64]{1,0:T(8,128)S(1)} %psum.23), channel_id=1, replica_groups=mesh['cuts'=4,'dev'=8] {'dev'}, dimensions={0}, use_global_device_ids=true | all-gather | bytes 147456 | tf_op jit(solution)/shard_map/all_gather | solution.py:35
  220.6 8.6 %fusion = bf16[1,3072,512]{2,1,0:T(8,128)(2,1)} fusion(f32[3072,512]{1,0:T(8,128)} %copy-done.1, f32[3072,64]{0,1:T(8,128)} %copy-done.2, f32[512,64]{1,0:T(8,128)S(1)} %all_gather.7), kind=kOutput, calls=%fused_computation.2 | convolution fusion | flops 1211138048 | bytes 10354688 | tf_op jit(solution)/shard_map/dot_general | solution.py:37
  229.2 0.8 copy.9
  230.0 2.1 copy.13
  (5 shorter events, 0.1 us)
Async XLA Ops:
  7.2 1.9 copy-start
  7.2 8.5 %copy-start.3 = (f32[512,64]{0,1:T(8,128)S(1)}, f32[512,64]{0,1:T(8,128)}, u32[]{:S(2)}) copy-start(f32[512,64]{0,1:T(8,128)} %param.7) | copy-start | bytes 393220
  7.2 53.5 %reduce-scatter.3.cloned.1.call-start = ((), (), s32[]{:S(2)}) async-start(), calls=%async_computation.2 | async-start | bytes 884736 | tf_op jit(solution)/shard_map/reduce_scatter | solution.py:26
  13.0 2.7 %copy-start.1 = (f32[3072,512]{1,0:T(8,128)}, f32[3072,512]{1,0:T(8,128)S(1)}, u32[]{:S(2)}) copy-start(f32[3072,512]{1,0:T(8,128)S(1)} %convert_add_fusion) | copy-start | bytes 18874372
  22.8 74.6 %all-reduce.2.cloned.1.call-start = ((), (), s32[]{:S(2)}) async-start(), calls=%async_computation.3 | async-start | bytes 196608 | tf_op jit(solution)/shard_map/psum | solution.py:29
  60.7 131.1 %reduce-scatter.5.cloned.1.call-start = ((), (), s32[]{:S(2)}) async-start(), calls=%async_computation.4 | async-start | bytes 294912 | tf_op jit(solution)/shard_map/reduce_scatter | solution.py:33
  145.5 0.9 copy-start.2
Sparse Core Ops, SparseCore 0:
  22.9 37.6 reduce-scatter.2
  63.0 34.4 all-reduce.1
  159.2 32.5 reduce-scatter.4
where the time goes:
time: 239 us
  waiting for transfers between devices  107 us (45%)
  blocking collectives  62.3 us (26%)
  matrix products  34.7 us (15%)
  between operations  13.8 us (6%)
  other arithmetic  12.1 us (5%)
  local copies, waits for them, and re-layouts  8.29 us (3%)
    reduce_scatter x1, waiting for transfers between devices, body(): lax.psum_scatter(jnp.dot(merged, previous_q, precision=HI), 'dev', scatte...  37.8 us
    psum x1, waiting for transfers between devices, body(): p_share = lax.psum(p_share, 'cuts')  36.7 us
    reduce_scatter x1, waiting for transfers between devices, body(): lax.psum_scatter(contract_rows(merged, p_hat), 'dev', scatter_dimension=0...  32.7 us
    psum x1, blocking collectives, body(): gram = lax.psum(contract_rows(p_share, p_share), 'dev')  22.4 us
    psum x1, blocking collectives, body(): q_share = lax.psum(q_share, 'cuts')  19.6 us
    dot_general x2, matrix products, contract_rows(): lax.dot_general(left, right, (((0,), (0,)), ((), ())), precision=HI, pref...  13.9 us
    all_gather x1, blocking collectives, body(): p_hat = lax.all_gather(hat_share, 'dev', axis=0, tiled=True)  11.1 us
    all_gather x1, blocking collectives, body(): q_sum = lax.all_gather(q_share, 'dev', axis=0, tiled=True)  9.24 us
  transfers between devices with their start and end apart: 3, of which 3 were waited for; matrix products, arithmetic and copies ran while one was open for 0% of the time, Pallas kernels for 0%

commit v1 on v0

--- a/solution.py
+++ b/solution.py
@@ -31,7 +31,7 @@
     hat_share = solve_factor(gram, p_share)
     p_hat = lax.all_gather(hat_share, "dev", axis=0, tiled=True)
     q_share = lax.psum_scatter(contract_rows(merged, p_hat), "dev", scatter_dimension=0, tiled=True)
-    q_share = lax.psum(q_share, "cuts")
+    q_share = lax.all_gather(q_share, "cuts").sum(axis=0)
     q_sum = lax.all_gather(q_share, "dev", axis=0, tiled=True)
     q_mean = q_sum / devices
     approx = jnp.dot(p_hat, q_mean.T, precision=HI)

time: 239 us -> 233 us (0.975)
  blocking collectives: 62.3 us -> 56.4 us
    psum x1 -> x0, blocking collectives: 19.6 us -> none  [body(): q_share = lax.psum(q_share, 'cuts')]
    all_gather x0 -> x1, blocking collectives: none -> 13.6 us  [body(): q_share = lax.all_gather(q_share, 'cuts').sum(axis=0)]
where the time goes in v1:
time: 233 us
  waiting for transfers between devices  107 us (46%)
  blocking collectives  56.4 us (24%)
  matrix products  34.7 us (15%)
  between operations  13.8 us (6%)
  other arithmetic  12.1 us (5%)
  local copies, waits for them, and re-layouts  8.29 us (4%)
    reduce_scatter x1, waiting for transfers between devices, body(): lax.psum_scatter(jnp.dot(merged, previous_q, precision=HI), 'dev', scatte...  37.8 us
    psum x1, waiting for transfers between devices, body(): p_share = lax.psum(p_share, 'cuts')  36.7 us
    reduce_scatter x1, waiting for transfers between devices, body(): lax.psum_scatter(contract_rows(merged, p_hat), 'dev', scatter_dimension=0...  32.7 us
    psum x1, blocking collectives, body(): gram = lax.psum(contract_rows(p_share, p_share), 'dev')  22.4 us
    dot_general x2, matrix products, contract_rows(): lax.dot_general(left, right, (((0,), (0,)), ((), ())), precision=HI, pref...  13.9 us
    all_gather x1, blocking collectives, body(): q_share = lax.all_gather(q_share, 'cuts').sum(axis=0)  13.6 us
    all_gather x1, blocking collectives, body(): p_hat = lax.all_gather(hat_share, 'dev', axis=0, tiled=True)  11.1 us
    all_gather x1, blocking collectives, body(): q_sum = lax.all_gather(q_share, 'dev', axis=0, tiled=True)  9.35 us
  transfers between devices with their start and end apart: 3, of which 3 were waited for; matrix products, arithmetic and copies ran while one was open for 0% of the time, Pallas kernels for 0%

profile of v1, /device:TPU:0, one launch (start us, length us, event | category | flops | bytes accessed | tf_op | source)
XLA Modules:
  0.0 232.7 jit_solution(7722686916687195156)
XLA Ops:
  7.2 0.0 copy-start
  7.2 0.0 copy-start.3
  7.2 0.0 reduce-scatter.3.cloned.1.call-start
  7.2 1.8 copy-done
  9.1 4.0 %convert_add_fusion = f32[3072,512]{1,0:T(8,128)S(1)} fusion(bf16[512,3072]{1,0:T(8,128)(2,1)S(1)} %copy-done, bf16[512,512]{1,0:T(8,128)(2,1)} %param.5, bf16[1,3072,512]{2,1,0:T(8,128)(2,1)} %param.6), kind=kOutput, calls=%fused_computation | convolution fusion | flops 1613758464 | bytes 13107200 | tf_op jit(solution)/shard_map/dot_general | solution.py:21
  13.1 2.7 %copy-done.1 = f32[3072,512]{1,0:T(8,128)} copy-done((f32[3072,512]{1,0:T(8,128)}, f32[3072,512]{1,0:T(8,128)S(1)}, u32[]{:S(2)}) %copy-start.1) | copy-done | bytes 6291480
  15.7 0.0 copy-done.3
  15.7 7.1 %fusion.5 = f32[3072,64]{0,1:T(8,128)} fusion(f32[3072,512]{1,0:T(8,128)S(1)} %convert_add_fusion, f32[512,64]{0,1:T(8,128)S(1)} %copy-done.3), kind=kOutput, calls=%fused_computation.14 | convolution fusion | flops 1207959552 | bytes 7208960 | tf_op jit(solution)/shard_map/dot_general | solution.py:27
  22.8 0.0 reduce-scatter.3.cloned.1.call-update
  22.8 0.0 all-reduce.2.cloned.1.call-start
  22.9 37.8 %reduce-scatter.3.cloned.1.call-done = f32[384,64]{0,1:T(8,128)} async-done(((f32[3072,64]{0,1:T(8,128)}), f32[384,64]{0,1:T(8,128)}) %reduce-scatter.3.cloned.1.call-update) | async-done | bytes 98320 | tf_op jit(solution)/shard_map/reduce_scatter | solution.py:26
  60.6 0.0 all-reduce.2.cloned.1.call-update
  60.7 0.0 reduce-scatter.5.cloned.1.call-start
  60.7 36.7 %all-reduce.2.cloned.1.call-done = f32[384,64]{0,1:T(8,128)} async-done(((f32[384,64]{0,1:T(8,128)}), f32[384,64]{0,1:T(8,128)}) %all-reduce.2.cloned.1.call-update) | async-done | bytes 98320 | tf_op jit(solution)/shard_map/psum | solution.py:29
  97.4 1.2 fusion.6
  98.7 22.4 %psum.15 = f32[64,64]{0,1:T(8,128)S(1)} all-reduce(f32[64,64]{0,1:T(8,128)S(1)} %fusion.6), channel_id=1, replica_groups=mesh['cuts'=4,'dev'=8] {'dev'}, use_global_device_ids=true, to_apply=%region_2.0 | all-reduce | flops 4096 | bytes 32768 | tf_op jit(solution)/shard_map/psum | solution.py:30
  121.0 0.1 copy.10
  121.1 5.8 %cholesky.16 = f32[64,64]{1,0:T(8,128)S(1)} custom-call(f32[64,64]{1,0:T(8,128)S(1)} %fusion.4), custom_call_target="Cholesky" | custom-call | tf_op jit(solution)/shard_map/jit(cholesky)/cholesky | solution.py:10
  127.0 0.6 compare_reduce_fusion
  127.6 0.7 fusion.1
  128.3 4.9 %custom-call.6 = f32[1,64,64]{1,2,0:T(8,128)S(1)} custom-call(f32[1,64,64]{2,1,0:T(8,128)S(1)} %fusion.1), custom_call_target="InvertDiagBlocksLowerTriangular" | custom-call | tf_op jit(solution)/shard_map/triangular_solve | solution.py:11
  133.2 1.2 fusion.2
  134.4 11.1 %all_gather.12 = f32[3072,64]{0,1:T(8,128)S(1)} all-gather(f32[384,64]{0,1:T(8,128)S(1)} %fusion.2), channel_id=1, replica_groups=mesh['cuts'=4,'dev'=8] {'dev'}, dimensions={0}, use_global_device_ids=true | all-gather | bytes 884736 | tf_op jit(solution)/shard_map/all_gather | solution.py:32
  145.5 0.9 copy-done.2
  146.4 12.7 %fusion.7 = f32[512,64]{1,0:T(8,128)} fusion(f32[3072,512]{1,0:T(8,128)} %copy-done.1, f32[3072,64]{0,1:T(8,128)S(1)} %all_gather.12), kind=kOutput, calls=%fused_computation.16 | convolution fusion | flops 1207959552 | bytes 7208960 | tf_op jit(solution)/shard_map/dot_general | solution.py:15
  159.1 0.0 reduce-scatter.5.cloned.1.call-update
  159.1 32.7 %reduce-scatter.5.cloned.1.call-done = f32[64,64]{1,0:T(8,128)} async-done(((f32[512,64]{1,0:T(8,128)}), f32[64,64]{1,0:T(8,128)}) %reduce-scatter.5.cloned.1.call-update) | async-done | bytes 16400 | tf_op jit(solution)/shard_map/reduce_scatter | solution.py:33
  191.8 13.6 %all-gather = f32[256,64]{1,0:T(8,128)S(1)} all-gather(f32[64,64]{1,0:T(8,128)} %reduce-scatter.5.cloned.1.call-done), channel_id=2, replica_groups=mesh['cuts'=4,'dev'=8] {'cuts'}, dimensions={0}, use_global_device_ids=true | all-gather | bytes 81920 | tf_op jit(solution)/shard_map/all_gather | solution.py:34
  205.4 9.4 %all_gather.15 = f32[512,64]{1,0:T(8,128)S(1)} all-gather(f32[64,64]{1,0:T(8,128)S(1)} %reduce_sum.9), channel_id=1, replica_groups=mesh['cuts'=4,'dev'=8] {'dev'}, dimensions={0}, use_global_device_ids=true | all-gather | bytes 147456 | tf_op jit(solution)/shard_map/all_gather | solution.py:35
  214.7 8.6 %fusion = bf16[1,3072,512]{2,1,0:T(8,128)(2,1)} fusion(f32[3072,512]{1,0:T(8,128)} %copy-done.1, f32[3072,64]{0,1:T(8,128)} %copy-done.2, f32[512,64]{1,0:T(8,128)S(1)} %all_gather.15), kind=kOutput, calls=%fused_computation.2 | convolution fusion | flops 1211138048 | bytes 10354688 | tf_op jit(solution)/shard_map/dot_general | solution.py:37
  223.3 0.8 copy.11
  224.1 2.1 copy.15
  (6 shorter events, 0.1 us)
Async XLA Ops:
  7.2 1.9 copy-start
  7.2 8.5 %copy-start.3 = (f32[512,64]{0,1:T(8,128)S(1)}, f32[512,64]{0,1:T(8,128)}, u32[]{:S(2)}) copy-start(f32[512,64]{0,1:T(8,128)} %param.7) | copy-start | bytes 393220
  7.2 53.5 %reduce-scatter.3.cloned.1.call-start = ((), (), s32[]{:S(2)}) async-start(), calls=%async_computation.2 | async-start | bytes 884736 | tf_op jit(solution)/shard_map/reduce_scatter | solution.py:26
  13.0 2.7 %copy-start.1 = (f32[3072,512]{1,0:T(8,128)}, f32[3072,512]{1,0:T(8,128)S(1)}, u32[]{:S(2)}) copy-start(f32[3072,512]{1,0:T(8,128)S(1)} %convert_add_fusion) | copy-start | bytes 18874372
  22.8 74.6 %all-reduce.2.cloned.1.call-start = ((), (), s32[]{:S(2)}) async-start(), calls=%async_computation.3 | async-start | bytes 196608 | tf_op jit(solution)/shard_map/psum | solution.py:29
  60.7 131.1 %reduce-scatter.5.cloned.1.call-start = ((), (), s32[]{:S(2)}) async-start(), calls=%async_computation.4 | async-start | bytes 294912 | tf_op jit(solution)/shard_map/reduce_scatter | solution.py:33
  145.5 0.9 copy-start.2
Sparse Core Ops, SparseCore 0:
  22.9 37.6 reduce-scatter.2
  63.0 34.4 all-reduce.1
  159.2 32.5 reduce-scatter.4
